TPU v7x, 32 devices: a whole 2x2x4 slice. The times are simulated.
32 devices in a mesh: row: 8 (over z, x), col: 4 (over y, core).
Axes of the slice: x: 2, y: 2, z: 4, core: 2. Of those that a mesh axis runs over, the one named last changes fastest.
Arguments:
- a_values: bfloat16 [2048, 2048], P('row', 'col'), may hold values from -0.125 to 0.125
- a_present: int32 [8, 8], P('row', 'col'), may hold values from 0 to 1, as said below
- b_values: bfloat16 [2048, 2048], P('row', 'col'), may hold values from -6 to 6
- b_present: int32 [8, 8], P('row', 'col'), may hold values 0 or 1
- w_values: bfloat16 [2048, 2048], P('row', 'col'), may hold values from -6 to 6
- w_present: int32 [8, 8], P('row', 'col'), may hold values 0 or 1
Outputs:
- masked: bfloat16 [2048, 2048], P('row', 'col')
- slot: float32 [8, 8], P('row', 'col')
- total: float32 [], replicated
Inputs may be any that keep to these rules, and one draw needn't show every extreme that they name: `a_present`: 1 where a tile of a_values is present, else 0; the share of present tiles differs strongly from tile row to tile row.
All inputs are finite; a program needn't handle non-finite values. No bound on the sum of `b_present` or of `w_present` on one device may be relied on, other than what follows from the above.
Results may differ from a plain program's by a relative error of at most 0.001.
Values may be sent and summed in bfloat16 or wider, within the bound.
A program may use at most 128 MiB of HBM per device.

v0:
```python
import math

import jax
import jax.numpy as jnp
from jax import lax
from jax.sharding import PartitionSpec as P

TILE = 256


def expand(values, present):
    tile_rows, tile_cols = present.shape
    tile_size = values.shape[0] // tile_rows
    blocked = values.reshape(tile_rows, tile_size, tile_cols, tile_size)
    masked_tiles = blocked * present.astype(values.dtype)[:, None, :, None]
    return masked_tiles.reshape(values.shape)


def on_device(a_values, a_present, b_values, b_present, w_values, w_present):
    tile_size = TILE
    row_tiles, inner_local = a_present.shape
    b_row_tiles, col_tiles = b_present.shape
    a_eff = expand(a_values, a_present)
    b_eff = expand(b_values, b_present).reshape(b_row_tiles, tile_size, col_tiles * tile_size)
    w_eff = expand(w_values, w_present).astype(jnp.float32)
    a_full, a_mask = (
        lax.all_gather(a_eff, "col", axis=1, tiled=True),
        lax.all_gather(a_present, "col", axis=1, tiled=True),
    )
    b_piece = lax.all_gather(b_eff, "row", axis=0, tiled=True)
    b_mask = lax.all_gather(b_present, "row", axis=0, tiled=True)
    count_tiles = b_mask.shape[0]
    new_prod = jnp.dot(
        a_full,
        b_piece.reshape(count_tiles * tile_size, col_tiles * tile_size),
        preferred_element_type=jnp.float32,
    )
    new_link = jnp.dot(a_mask, b_mask, preferred_element_type=jnp.int32)
    weighted = new_prod * w_eff
    masked = weighted.astype(jnp.bfloat16)
    local_sum = jnp.sum(weighted)
    present = w_present * (new_link > 0).astype(jnp.int32)
    flat_present = present.reshape(-1)
    tile_count = jnp.sum(flat_present)
    tile_rank = jnp.cumsum(flat_present) - flat_present
    counts_all, sums_all = (
        lax.all_gather(tile_count.astype(jnp.float32)[None], ("row", "col"), axis=0, tiled=True),
        lax.all_gather(local_sum[None], ("row", "col"), axis=0, tiled=True),
    )
    position = lax.axis_index(("row", "col"))
    earlier_mask = jnp.arange(counts_all.shape[0], dtype=jnp.int32) < position
    first_slot = jnp.sum(jnp.where(earlier_mask, counts_all, 0.0)).astype(jnp.int32)
    whole_sum = jnp.sum(sums_all)
    slot = jnp.where(flat_present > 0, first_slot + tile_rank, -1).reshape(row_tiles, col_tiles)
    norm_scale = tile_size * math.sqrt(
        row_tiles * lax.axis_size("row") * col_tiles * lax.axis_size("col")
    )
    total = whole_sum / norm_scale
    return (masked, slot.astype(jnp.float32), total)


def solution(mesh):
    in_specs = (
        P("row", "col"),
        P("row", "col"),
        P("row", "col"),
        P("row", "col"),
        P("row", "col"),
        P("row", "col"),
    )
    out_specs = (P("row", "col"), P("row", "col"), P())
    return jax.shard_map(
        on_device, mesh=mesh, in_specs=in_specs, out_specs=out_specs, check_vma=False
    )
```

profile of v0, /device:TPU:0, one launch (start us, length us, event | category | flops | bytes accessed | tf_op | source)
XLA Modules:
  0.0 135.7 jit_solution(8111661884255417502)
XLA Ops:
  7.2 0.0 all-gather.5.cloned.1.call-start
  7.2 0.7 convert_bitcast_fusion.2
  7.9 0.1 broadcast_bitcast_fusion.2
  8.0 1.7 %broadcast_multiply_fusion.1 = bf16[256,512]{1,0:T(8,128)(2,1)} fusion(bf16[256,512]{1,0:T(8,128)(2,1)} %param.6, bf16[512]{0:T(512)(128)(2,1)S(1)} %bitcast.44), kind=kLoop, calls=%fused_computation.6 | loop fusion | flops 131072 | bytes 525312 | tf_op jit(solution)/shard_map/mul | solution.py:15
  9.6 0.0 all-gather.5.cloned.1.call-update
  9.7 0.0 all-gather.7.cloned.1.call-start
  9.7 0.7 convert_bitcast_fusion.1
  10.4 0.1 broadcast_bitcast_fusion.1
  10.4 1.7 %broadcast_multiply_fusion = bf16[256,512]{1,0:T(8,128)(2,1)} fusion(bf16[256,512]{1,0:T(8,128)(2,1)} %param.8, bf16[512]{0:T(512)(128)(2,1)S(1)} %bitcast.45), kind=kLoop, calls=%fused_computation.5 | loop fusion | flops 131072 | bytes 525312 | tf_op jit(solution)/shard_map/mul | solution.py:15
  12.1 0.0 all-gather.7.cloned.1.call-update
  12.2 1.2 dynamic-slice
  14.1 0.8 bitcast_dynamic-update-slice_fusion
  14.8 22.4 %all-gather.1 = s32[8,1,2]{2,1,0:T(1,128)S(1)} all-gather(s32[1,1,2]{2,1,0:T(1,128)} %bitcast.47), channel_id=1, replica_groups=mesh['row'=8,'col'=4] {'row'}, dimensions={0}, use_global_device_ids=true | all-gather | bytes 72 | tf_op jit(solution)/shard_map/all_gather | solution.py:31
  37.2 4.9 %all-reduce = s32[8]{0:T(128)S(1)} all-reduce(s32[8]{0:T(128)S(1)} %bitcast_dynamic-update-slice_fusion), channel_id=1, replica_groups=mesh['row'=8,'col'=4] {'col'}, use_global_device_ids=true, to_apply=%add | all-reduce | flops 8 | bytes 64 | tf_op jit(solution)/shard_map/reshape.5
  42.2 0.7 convert_bitcast_fusion
  42.8 0.1 broadcast_bitcast_fusion
  42.9 1.4 %fusion.7 = (s32[]{:T(128)}, s32[1,2]{1,0:T(1,128)S(1)}) fusion(s32[1,2]{1,0:T(1,128)} %param.11, s32[8,2]{1,0:T(8,128)S(1)} %bitcast.43, s32[8]{0:T(128)S(1)} %all-reduce), kind=kOutput, calls=%fused_computation.20 | convolution fusion | flops 37 | bytes 116 | tf_op jit(solution)/shard_map/dot_general | solution.py:38
  44.3 0.2 reduce-window_clone.1
  45.2 0.1 dynamic-update-slice.1
  45.3 0.0 all-gather.5.cloned.1.call-done
  45.3 35.6 %all-gather.7.cloned.1.call-done = bf16[2048,512]{1,0:T(8,128)(2,1)} async-done(((bf16[256,512]{1,0:T(8,128)(2,1)}), bf16[2048,512]{1,0:T(8,128)(2,1)}) %all-gather.7.cloned.1.call-update) | async-done | bytes 2097168 | tf_op jit(solution)/shard_map/all_gather | solution.py:30
  80.9 3.9 %fusion.6 = (f32[]{:T(128)}, bf16[256,512]{1,0:T(8,128)(2,1)}) fusion(bf16[256,512]{1,0:T(8,128)(2,1)} %param.10, bf16[512]{0:T(512)(128)(2,1)S(1)} %bitcast.46, bf16[256,2048]{1,0:T(8,128)(2,1)} %all-gather.5.cloned.1.call-done, bf16[2048,512]{1,0:T(8,128)(2,1)} %all-gather.7.cloned.1.call-done), kind=kOutput, calls=%fused_computation.19 | convolution fusion | flops 537526272 | bytes 3671044 | tf_op jit(solution)/shard_map/dot_general | solution.py:33
  84.8 0.8 dynamic-update-slice.2
  85.5 39.2 %all-reduce.3 = (f32[32]{0:T(128)S(1)}, f32[32]{0:T(128)S(1)}) all-reduce(f32[32]{0:T(128)S(1)} %dynamic-update-slice.1, f32[32]{0:T(128)S(1)} %dynamic-update-slice.2), channel_id=1, replica_groups=mesh['row'=8,'col'=4] {'row','col'}, use_global_device_ids=true, to_apply=%add.1 | all-reduce | flops 64 | bytes 512
  124.7 0.6 fusion.4
  126.0 0.5 fusion.3
  126.5 0.6 reduce_sum.39
  (6 shorter events, 0.0 us)
Async XLA Ops:
  7.2 38.1 %all-gather.5.cloned.1.call-start = ((), (), s32[]{:S(2)}) async-start(), calls=%async_computation | async-start | bytes 1310720 | tf_op jit(solution)/shard_map/all_gather | solution.py:27
  9.7 71.2 %all-gather.7.cloned.1.call-start = ((), (), s32[]{:S(2)}) async-start(), calls=%async_computation.1 | async-start | bytes 2359296 | tf_op jit(solution)/shard_map/all_gather | solution.py:30
Sparse Core Ops, SparseCore 0:
  10.1 19.4 all-gather.4
  31.7 49.1 all-gather.6
where the time goes:
time: 136 us
  blocking collectives  66.5 us (49%)
  waiting for transfers between devices  35.6 us (26%)
  between operations  17.8 us (13%)
  other arithmetic  7.23 us (5%)
  matrix products  5.33 us (4%)
  local copies, waits for them, and re-layouts  3.12 us (2%)
    unnamed x1, blocking collectives  39.2 us
    all_gather x1, waiting for transfers between devices, on_device(): b_piece = lax.all_gather(b_eff, 'row', axis=0, tiled=True)  35.6 us
    all_gather x1, blocking collectives, on_device(): b_mask = lax.all_gather(b_present, 'row', axis=0, tiled=True)  22.4 us
    mul x5, other arithmetic, expand(): masked_tiles = blocked * present.astype(values.dtype)[:, None, :, None]  5.34 us
    another operation x1, blocking collectives  4.93 us
    dot_general x1, matrix products, on_device(): jnp.dot(a_full, b_piece.reshape(count_tiles * tile_size, col_tiles * tile...  3.9 us
    unnamed x13, local copies, waits for them, and re-layouts  3.12 us
  transfers between devices with their start and end apart: 2, of which 1 were waited for; matrix products, arithmetic and copies ran while one was open for 5% of the time, Pallas kernels for 0%

commit v1 on v0

v1 whole, which is shorter than its diff:
```python
import functools
import math

import jax
import jax.numpy as jnp
from jax import lax
from jax.experimental import pallas as pl
from jax.experimental.pallas import tpu as pltpu
from jax.sharding import PartitionSpec as P

MESH = pl.DeviceIdType.MESH
PIECES = 4


class Gather:
    def __init__(self, axis, n, buf, send_sem, recv_sem, pieces, diverted):
        self.axis, self.buf = axis, buf
        self.send_sem, self.recv_sem = send_sem, recv_sem
        self.me = lax.axis_index(axis)
        self.length = n // 2
        self.place, self.side = self.me // 2, self.me % 2
        self.pieces = pieces
        self.height = buf.shape[1] // pieces
        self.diverted = tuple(range(pieces - pieces // 2, pieces)) if diverted else ()

    def copy(self, way, slot, h):
        target = (self.me + 2, self.me - 2, self.me + 1 - 2 * self.side)[way]
        part = self.buf.at[slot, pl.ds(h * self.height, self.height), :]
        return pltpu.make_async_remote_copy(
            src_ref=part,
            dst_ref=part,
            send_sem=self.send_sem.at[way, slot, h],
            recv_sem=self.recv_sem.at[slot, h],
            device_id={self.axis: target},
            device_id_type=MESH,
        )

    def can_up(self):
        return self.place < self.length - 1

    def can_down(self):
        return self.place > 0

    def when_all(self, *conds):
        return pl.when(functools.reduce(jnp.logical_and, conds))

    def run(self, action, way, slot, h, *conds):
        @self.when_all(*conds)
        def _():
            action(self.copy(way, slot, h))

    def own(self, action):
        for h in range(self.pieces):
            self.run(action, 0, self.me, h, self.can_up())
            self.run(action, 1, self.me, h, self.can_down())
            action(self.copy(2, self.me, h))

    def line(self, d, receive, action):
        last = self.length - 1
        for h in range(self.pieces):
            for way, source, onward, end in (
                (0, self.place - d, self.can_up, 0),
                (1, self.place + d, self.can_down, last),
            ):
                slot = 2 * source + self.side
                there = jnp.logical_and(source >= 0, source <= last)
                if receive:
                    self.run(lambda c: c.wait_recv(), 2, slot, h, there)
                self.run(action, way, slot, h, there, onward())
                if h in self.diverted:
                    self.run(action, 2, slot, h, there, source != end)
                else:
                    self.run(action, 2, slot, h, there)

    def divert(self, d, receive, action):
        last = self.length - 1
        for h in self.diverted:
            for way, source, at, onward in (
                (0, 0, d, self.can_up),
                (1, last, last - d, self.can_down),
            ):
                slot = 2 * source + 1 - self.side
                here = self.place == at
                if receive:
                    self.run(lambda c: c.wait_recv(), 2, slot, h, here)
                self.run(action, way, slot, h, here, onward())

    def across(self, d):
        last = self.length - 1
        for h in range(self.pieces):
            for step, end in ((-1, 0), (1, last)):
                source = self.place + step * d
                slot = 2 * source + 1 - self.side
                there = jnp.logical_and(source >= 0, source <= last)
                if step > 0:
                    there = jnp.logical_and(there, d > 0)
                if h in self.diverted:
                    there = jnp.logical_and(there, jnp.logical_and(source != 0, source != last))
                self.run(lambda c: c.wait_recv(), 2, slot, h, there)


def start(c):
    c.start()


def wait_send(c):
    c.wait_send()


def kernel(
    n_row, n_col, tr, ka, br, tc, tile, scale,
    a_hbm, b_hbm, w_hbm, ap_ref, bp_ref, wp_ref,
    masked_hbm, slot_ref, total_ref,
    abuf, bbuf, wbuf, acc, obuf, amask, bmask, gate, ex,
    local_sem, a_send, a_recv, b_send, b_recv, am_send, am_recv, bm_send, bm_recv, ex_send, ex_recv,
):
    row, col = lax.axis_index("row"), lax.axis_index("col")
    me = row * n_col + col
    everyone = n_row * n_col
    ga = Gather("col", n_col, abuf, a_send, a_recv, min(PIECES, 2), False)
    gb = Gather("row", n_row, bbuf, b_send, b_recv, PIECES, True)

    loads = [
        pltpu.make_async_copy(b_hbm, bbuf.at[row], local_sem.at[0]),
        pltpu.make_async_copy(a_hbm, abuf.at[col], local_sem.at[1]),
        pltpu.make_async_copy(w_hbm, wbuf, local_sem.at[2]),
    ]
    for load in loads:
        load.start()

    barrier = pltpu.get_barrier_semaphore()

    def greet(o, _):
        other = lax.rem(me + o, everyone)
        pl.semaphore_signal(
            barrier, inc=1, device_id=(other // n_col, lax.rem(other, n_col)), device_id_type=MESH
        )
        return 0

    lax.fori_loop(1, everyone, greet, 0)

    lane = lax.broadcasted_iota(jnp.int32, (1, 128), 1)

    def packed(ref, rows, cols):
        v = jnp.zeros((1, 128), jnp.int32)
        for i in range(rows):
            for j in range(cols):
                v = jnp.where(lane == i * cols + j, ref[i : i + 1, j : j + 1], v)
        return v

    amask[col] = packed(ap_ref, tr, ka)
    bmask[row] = packed(bp_ref, br, tc)
    acc[...] = jnp.zeros_like(acc)
    pl.semaphore_wait(barrier, everyone - 1)

    def mask_copy(axis, mine, buf, send, recv, o, n):
        other = lax.rem(mine + o, n)
        return pltpu.make_async_remote_copy(
            src_ref=buf.at[mine], dst_ref=buf.at[mine],
            send_sem=send.at[other], recv_sem=recv.at[mine],
            device_id={axis: other}, device_id_type=MESH,
        )

    def mask_arrival(axis, mine, buf, send, recv, o, n):
        other = lax.rem(mine + o, n)
        return pltpu.make_async_remote_copy(
            src_ref=buf.at[other], dst_ref=buf.at[other],
            send_sem=send.at[other], recv_sem=recv.at[other],
            device_id={axis: other}, device_id_type=MESH,
        )

    mask_sets = (
        ("col", col, amask, am_send, am_recv, n_col),
        ("row", row, bmask, bm_send, bm_recv, n_row),
    )

    def masks(make, action):
        for axis, mine, buf, send, recv, n in mask_sets:
            def one(o, _):
                action(make(axis, mine, buf, send, recv, o, n))
                return 0
            lax.fori_loop(1, n, one, 0)

    loads[0].wait()
    gb.own(start)
    loads[1].wait()
    ga.own(start)
    masks(mask_copy, start)
    loads[2].wait()

    def lane_row(v, j):
        return jnp.broadcast_to(v[:, j : j + 1], (1, tile))

    def prepare():
        masks(mask_arrival, lambda c: c.wait_recv())
        links = [jnp.zeros((1, tc * tile), jnp.int32) for _ in range(tr)]
        for k in range(ka * n_col):
            bv = bmask[k // br]
            brow = jnp.concatenate([lane_row(bv, (k % br) * tc + j) for j in range(tc)], axis=1)
            av = amask[k // ka]
            for i in range(tr):
                at = i * ka + k % ka
                g = av[:, at : at + 1] * brow
                gate[k * tr + i] = g.astype(jnp.float32)
                links[i] = links[i] + g
        for i in range(tr):
            wrow = jnp.concatenate(
                [jnp.broadcast_to(wp_ref[i : i + 1, j : j + 1], (1, tile)) for j in range(tc)], axis=1
            )
            gate[ka * n_col * tr + i] = wrow.astype(jnp.float32)
            gate[ka * n_col * tr + tr + i] = jnp.where(links[i] > 0, wrow, 0).astype(jnp.float32)
        def a_step(d, _):
            ga.line(d, True, start)
            return 0
        lax.fori_loop(1, n_col // 2, a_step, 0)
        def a_across(d, _):
            ga.across(d)
            return 0
        lax.fori_loop(0, n_col // 2, a_across, 0)

    def compute(slot):
        for bi in range(br):
            k = slot * br + bi
            dev = k // ka
            lanes = pl.ds(pl.multiple_of(lax.rem(k, ka) * tile, tile), tile)
            block = bbuf[slot, bi * tile : (bi + 1) * tile, :]
            for i in range(tr):
                rows = slice(i * tile, (i + 1) * tile)
                g = gate[k * tr + i].astype(jnp.bfloat16)
                acc[rows, :] += jnp.dot(
                    abuf[dev, rows, lanes], block * g, preferred_element_type=jnp.float32
                )

    half = gb.length

    def step(d, _):
        gb.line(d, True, start)

        @pl.when(d == 1)
        def _():
            gb.divert(0, True, start)
            prepare()

        gb.divert(d, True, start)

        def near(j, _):
            place = gb.place + jnp.where(j == 0, 0, jnp.where(j == 1, -d, d))
            there = jnp.logical_and(place >= 0, place < half)
            there = jnp.logical_and(there, jnp.logical_or(j > 0, d == 1))
            there = jnp.logical_and(there, jnp.logical_or(j == 0, d < half))

            @pl.when(there)
            def _():
                compute(2 * place + gb.side)
            return 0

        lax.fori_loop(0, 3, near, 0)
        gb.across(d - 1)

        def far(j, _):
            place = gb.place + jnp.where(j == 0, 1 - d, d - 1)
            there = jnp.logical_and(place >= 0, place < half)
            there = jnp.logical_and(there, jnp.logical_or(j == 0, d > 1))

            @pl.when(there)
            def _():
                compute(2 * place + 1 - gb.side)
            return 0

        lax.fori_loop(0, 2, far, 0)
        return 0

    lax.fori_loop(1, half + 1, step, 0)

    base = ka * n_col * tr
    part = jnp.zeros((1, tc * tile), jnp.float32)
    for i in range(tr):
        rows = slice(i * tile, (i + 1) * tile)
        weighted = acc[rows, :] * (wbuf[rows, :].astype(jnp.float32) * gate[base + i])
        obuf[rows, :] = weighted.astype(jnp.bfloat16)
        part = part + jnp.sum(weighted, axis=0, keepdims=True)
    local_sum = jnp.sum(part, axis=1, keepdims=True)
    count = jnp.zeros((1, 1), jnp.float32)
    for i in range(tr):
        for j in range(tc):
            count = count + gate[base + tr + i][:, j * tile : j * tile + 1]
    ex[me] = jnp.where(lane == 0, local_sum, jnp.where(lane == 1, count, 0.0))

    def ex_copy(o, mine):
        other = lax.rem(me + o, everyone)
        slot = me if mine else other
        return pltpu.make_async_remote_copy(
            src_ref=ex.at[slot], dst_ref=ex.at[slot],
            send_sem=ex_send.at[other], recv_sem=ex_recv.at[slot],
            device_id=(other // n_col, lax.rem(other, n_col)), device_id_type=MESH,
        )

    def ex_start(o, _):
        ex_copy(o, True).start()
        return 0

    def ex_wait(o, _):
        ex_copy(o, False).wait_recv()
        return 0

    def ex_done(o, _):
        ex_copy(o, True).wait_send()
        return 0

    lax.fori_loop(1, everyone, ex_start, 0)
    store = pltpu.make_async_copy(obuf, masked_hbm, local_sem.at[3])
    store.start()

    gb.own(wait_send)
    ga.own(wait_send)
    masks(mask_copy, wait_send)

    def drain_b(d, _):
        gb.line(d, False, wait_send)
        gb.divert(d, False, wait_send)
        return 0

    gb.divert(0, False, wait_send)
    lax.fori_loop(1, half + 1, drain_b, 0)

    def drain_a(d, _):
        ga.line(d, False, wait_send)
        return 0

    lax.fori_loop(1, n_col // 2, drain_a, 0)

    lax.fori_loop(1, everyone, ex_wait, 0)
    sums, first = jnp.zeros((1, 128), jnp.float32), jnp.zeros((1, 128), jnp.float32)
    everything = ex[...]
    order = lax.broadcasted_iota(jnp.int32, (everyone, 1, 128), 0)
    sums = jnp.sum(everything, axis=0)
    first = jnp.sum(jnp.where(order < me, everything, 0.0), axis=0)
    total_ref[...] = sums[:, 0:1] / scale
    before = first[:, 1:2]
    for i in range(tr):
        for j in range(tc):
            there = gate[base + tr + i][:, j * tile : j * tile + 1]
            slot_ref[i : i + 1, j : j + 1] = jnp.where(there > 0, before, -1.0)
            before = before + there
    lax.fori_loop(1, everyone, ex_done, 0)
    store.wait()


def on_device(a_values, a_present, b_values, b_present, w_values, w_present):
    n_row, n_col = lax.axis_size("row"), lax.axis_size("col")
    tr, ka = a_present.shape
    br, tc = b_present.shape
    tile = a_values.shape[0] // tr
    kt = ka * n_col
    scale = tile * math.sqrt(tr * n_row * tc * n_col)
    everyone = n_row * n_col
    dma = pltpu.SemaphoreType.DMA
    hbm = pl.BlockSpec(memory_space=pl.ANY)
    vmem = pl.BlockSpec(memory_space=pltpu.VMEM)
    masked, slot, total = pl.pallas_call(
        functools.partial(kernel, n_row, n_col, tr, ka, br, tc, tile, scale),
        out_shape=(
            jax.ShapeDtypeStruct(w_values.shape, jnp.bfloat16),
            jax.ShapeDtypeStruct((tr, tc), jnp.float32),
            jax.ShapeDtypeStruct((1, 1), jnp.float32),
        ),
        in_specs=[hbm, hbm, hbm, vmem, vmem, vmem],
        out_specs=(hbm, vmem, vmem),
        scratch_shapes=[
            pltpu.VMEM((n_col, *a_values.shape), jnp.bfloat16),
            pltpu.VMEM((n_row, *b_values.shape), jnp.bfloat16),
            pltpu.VMEM(w_values.shape, jnp.bfloat16),
            pltpu.VMEM(w_values.shape, jnp.float32),
            pltpu.VMEM(w_values.shape, jnp.bfloat16),
            pltpu.VMEM((n_col, 1, 128), jnp.int32),
            pltpu.VMEM((n_row, 1, 128), jnp.int32),
            pltpu.VMEM((kt * tr + 2 * tr, 1, tc * tile), jnp.float32),
            pltpu.VMEM((everyone, 1, 128), jnp.float32),
            dma((4,)),
            dma((3, n_col, PIECES)),
            dma((n_col, PIECES)),
            dma((3, n_row, PIECES)),
            dma((n_row, PIECES)),
            dma((n_col,)),
            dma((n_col,)),
            dma((n_row,)),
            dma((n_row,)),
            dma((everyone,)),
            dma((everyone,)),
        ],
        compiler_params=pltpu.CompilerParams(
            collective_id=0, has_side_effects=True, vmem_limit_bytes=56 * 1024 * 1024
        ),
    )(a_values, b_values, w_values, a_present, b_present, w_present)
    return masked, slot, total.reshape(())


def solution(mesh):
    spec = P("row", "col")
    return jax.shard_map(
        on_device, mesh=mesh, in_specs=(spec,) * 6, out_specs=(spec, spec, P()), check_vma=False
    )
```

time: 136 us -> 43 us (0.32)
  blocking collectives: 66.5 us -> 0 us
  Pallas kernels: 0 us -> 38.2 us
  waiting for transfers between devices: 35.6 us -> 0 us
  between operations: 17.8 us -> 2.47 us
  other arithmetic: 7.23 us -> 0 us
  matrix products: 5.33 us -> 0 us
    unnamed x1 -> x0, blocking collectives: 39.2 us -> none
    pallas_call x0 -> x1, Pallas kernels: none -> 38.2 us  [on_device(): pl.pallas_call(functools.partial(kernel, n_row, n_col, tr, ka, br, tc, ti...]
    all_gather x2 -> x0, waiting for transfers between devices: 35.6 us -> none  [the longest x1 35.6 us: on_device(): b_piece = lax.all_gather(b_eff, 'row', axis=0, tiled=True)]
    all_gather x1 -> x0, blocking collectives: 22.4 us -> none  [on_device(): b_mask = lax.all_gather(b_present, 'row', axis=0, tiled=True)]
    mul x5 -> x0, other arithmetic: 5.34 us -> none  [expand(): masked_tiles = blocked * present.astype(values.dtype)[:, None, :, None]]
    dot_general x2 -> x0, matrix products: 5.33 us -> none  [the longest x1 3.9 us: on_device(): jnp.dot(a_full, b_piece.reshape(count_tiles * tile_size, col_tiles * tile...]
    another operation x1 -> x0, blocking collectives: 4.93 us -> none
    unnamed x13 -> x4, local copies, waits for them, and re-layouts: 3.12 us -> 2.18 us
  transfers between devices with their start and end apart: 2 -> 0, of which waited for: 1 -> 0; matrix products, arithmetic and copies ran while one was open for 5% -> 0% of each run, Pallas kernels for 0% -> 0%
where the time goes in v1:
time: 43 us; the launch traced here: 42.8 us
  Pallas kernels  38.2 us (89%)
  between operations  2.47 us (6%)
  local copies, waits for them, and re-layouts  2.18 us (5%)
    pallas_call x1, Pallas kernels, on_device(): pl.pallas_call(functools.partial(kernel, n_row, n_col, tr, ka, br, tc, ti...  38.2 us
    unnamed x4, local copies, waits for them, and re-layouts  2.18 us

profile of v1, /device:TPU:0, one launch (start us, length us, event | category | flops | bytes accessed | tf_op | source)
XLA Modules:
  0.0 42.8 jit_solution(6494801030038163404)
XLA Ops:
  0.6 38.2 %shard_map.85 = (bf16[256,512]{1,0:T(8,128)(2,1)}, f32[1,2]{1,0:T(1,128)}, f32[1,1]{1,0:T(1,128)}) custom-call(bf16[256,512]{1,0:T(8,128)(2,1)} %a_hbm.1, bf16[256,512]{1,0:T(8,128)(2,1)} %b_hbm.1, bf16[256,512]{1,0:T(8,128)(2,1)} %w_hbm.1, s32[1,2]{1,0:T(1,128)} %ap_ref.1, s32[1,2]{1,0:T(1,128)} %bp_ref.1, s32[1,2]{1,0:T(1,128)} %wp_ref.1), custom_call_target="tpu_custom_call" | custom-call | tf_op jit(solution)/shard_map/pallas_call | solution.py:360
  38.8 0.0 copy-start
  38.8 1.7 %copy.12 = bf16[256,512]{1,0:T(8,128)(2,1)} copy(bf16[256,512]{1,0:T(8,128)(2,1)} %get-tuple-element.12) | data formatting | bytes 524288
  40.5 0.0 copy-done
  40.5 0.5 %copy.13 = f32[1,2]{1,0:T(1,128)} copy(f32[1,2]{1,0:T(1,128)S(1)} %copy-done) | data formatting | bytes 16
Async XLA Ops:
  38.8 1.7 %copy-start = (f32[1,2]{1,0:T(1,128)S(1)}, f32[1,2]{1,0:T(1,128)}, u32[]{:S(2)}) copy-start(f32[1,2]{1,0:T(1,128)} %get-tuple-element.13) | copy-start | bytes 28

commit v2 on v1

--- a/solution.py
+++ b/solution.py
@@ -9,7 +9,8 @@
 from jax.sharding import PartitionSpec as P
 
 MESH = pl.DeviceIdType.MESH
-PIECES = 4
+PIECES = 2
+A_PIECES = 2
 
 
 class Gather:
@@ -109,114 +110,133 @@
 
 def kernel(
     n_row, n_col, tr, ka, br, tc, tile, scale,
-    a_hbm, b_hbm, w_hbm, ap_ref, bp_ref, wp_ref,
-    masked_hbm, slot_ref, total_ref,
-    abuf, bbuf, wbuf, acc, obuf, amask, bmask, gate, ex,
-    local_sem, a_send, a_recv, b_send, b_recv, am_send, am_recv, bm_send, bm_recv, ex_send, ex_recv,
+    a_hbm, b_hbm, w_hbm, ap_hbm, bp_hbm, wp_hbm,
+    obuf, slot_ref, total_ref,
+    abuf, bbuf, wbuf, acc, ap_ref, bp_ref, wp_ref, amask, bmask, ex,
+    local_sem, a_send, a_recv, b_send, b_recv, am_send, am_recv, bm_send, bm_recv, ex_send, ex_recv, token,
 ):
     row, col = lax.axis_index("row"), lax.axis_index("col")
     me = row * n_col + col
     everyone = n_row * n_col
-    ga = Gather("col", n_col, abuf, a_send, a_recv, min(PIECES, 2), False)
+    ga = Gather("col", n_col, abuf, a_send, a_recv, A_PIECES, False)
     gb = Gather("row", n_row, bbuf, b_send, b_recv, PIECES, True)
 
-    loads = [
-        pltpu.make_async_copy(b_hbm, bbuf.at[row], local_sem.at[0]),
-        pltpu.make_async_copy(a_hbm, abuf.at[col], local_sem.at[1]),
-        pltpu.make_async_copy(w_hbm, wbuf, local_sem.at[2]),
-    ]
+    pairs = (
+        (bp_hbm, bp_ref), (b_hbm, bbuf.at[row]), (ap_hbm, ap_ref),
+        (a_hbm, abuf.at[col]), (wp_hbm, wp_ref), (w_hbm, wbuf),
+    )
+    loads = [pltpu.make_async_copy(x, y, local_sem.at[i]) for i, (x, y) in enumerate(pairs)]
     for load in loads:
         load.start()
 
+    def signal(sem, g, shift):
+        pl.semaphore_signal(sem, inc=1, device_id={g.axis: g.me + shift}, device_id_type=MESH)
+
     barrier = pltpu.get_barrier_semaphore()
-
-    def greet(o, _):
-        other = lax.rem(me + o, everyone)
-        pl.semaphore_signal(
-            barrier, inc=1, device_id=(other // n_col, lax.rem(other, n_col)), device_id_type=MESH
-        )
-        return 0
-
-    lax.fori_loop(1, everyone, greet, 0)
-
-    lane = lax.broadcasted_iota(jnp.int32, (1, 128), 1)
-
-    def packed(ref, rows, cols):
-        v = jnp.zeros((1, 128), jnp.int32)
+    greeted = 0
+    for g in (gb, ga):
+        signal(barrier, g, 1 - 2 * g.side)
+        pl.when(g.can_up())(functools.partial(signal, barrier, g, 2))
+        pl.when(g.can_down())(functools.partial(signal, barrier, g, -2))
+        greeted += 1 + g.can_up().astype(jnp.int32) + g.can_down().astype(jnp.int32)
+
+    def gated(get, put, present, rows, cols):
         for i in range(rows):
             for j in range(cols):
-                v = jnp.where(lane == i * cols + j, ref[i : i + 1, j : j + 1], v)
-        return v
-
-    amask[col] = packed(ap_ref, tr, ka)
-    bmask[row] = packed(bp_ref, br, tc)
-    acc[...] = jnp.zeros_like(acc)
-    pl.semaphore_wait(barrier, everyone - 1)
-
-    def mask_copy(axis, mine, buf, send, recv, o, n):
-        other = lax.rem(mine + o, n)
-        return pltpu.make_async_remote_copy(
-            src_ref=buf.at[mine], dst_ref=buf.at[mine],
-            send_sem=send.at[other], recv_sem=recv.at[mine],
-            device_id={axis: other}, device_id_type=MESH,
-        )
-
-    def mask_arrival(axis, mine, buf, send, recv, o, n):
-        other = lax.rem(mine + o, n)
-        return pltpu.make_async_remote_copy(
-            src_ref=buf.at[other], dst_ref=buf.at[other],
-            send_sem=send.at[other], recv_sem=recv.at[other],
-            device_id={axis: other}, device_id_type=MESH,
-        )
+                m = present[i : i + 1, j : j + 1].astype(jnp.float32).astype(jnp.bfloat16)
+                put(i, j, get(i, j) * m)
+
+    def gate_block(buf, slot, present, rows, cols):
+        def part(i, j):
+            return (slot, slice(i * tile, (i + 1) * tile), slice(j * tile, (j + 1) * tile))
+
+        def put(i, j, v):
+            buf[part(i, j)] = v
+
+        gated(lambda i, j: buf[part(i, j)], put, present, rows, cols)
+
+    loads[0].wait()
+    loads[1].wait()
+    gate_block(bbuf, row, bp_ref, br, tc)
+    loads[2].wait()
+    loads[3].wait()
+    gate_block(abuf, col, ap_ref, tr, ka)
+    pl.semaphore_wait(barrier, greeted)
+    gb.own(start)
+    ga.own(start)
+
+    for i, g in enumerate((ga, gb)):
+        pair, up, down = token.at[3 * i], token.at[3 * i + 1], token.at[3 * i + 2]
+        signal(pair, g, 1 - 2 * g.side)
+        if i == 0:
+            lane = lax.broadcasted_iota(jnp.int32, (1, 128), 1)
+
+            def packed(ref, rows, cols):
+                v = jnp.zeros((1, 128), jnp.int32)
+                for r in range(rows):
+                    for c in range(cols):
+                        v = jnp.where(lane == r * cols + c, ref[r : r + 1, c : c + 1], v)
+                return v
+
+            amask[col] = packed(ap_ref, tr, ka)
+            bmask[row] = packed(bp_ref, br, tc)
+        pl.semaphore_wait(pair, 1)
+        last = g.length - 1
+        first_up = jnp.logical_and(g.place == 0, g.can_up())
+        first_down = jnp.logical_and(g.place == last, g.can_down())
+        pl.when(first_up)(functools.partial(signal, up, g, 2))
+        pl.when(first_down)(functools.partial(signal, down, g, -2))
+        if i == 0:
+            acc[...] = jnp.zeros_like(acc)
+
+        @pl.when(g.can_down())
+        def _():
+            pl.semaphore_wait(up, 1)
+            pl.when(g.can_up())(functools.partial(signal, up, g, 2))
+
+        @pl.when(g.can_up())
+        def _():
+            pl.semaphore_wait(down, 1)
+            pl.when(g.can_down())(functools.partial(signal, down, g, -2))
 
     mask_sets = (
         ("col", col, amask, am_send, am_recv, n_col),
         ("row", row, bmask, bm_send, bm_recv, n_row),
     )
 
-    def masks(make, action):
+    def masks(arriving, action):
         for axis, mine, buf, send, recv, n in mask_sets:
             def one(o, _):
-                action(make(axis, mine, buf, send, recv, o, n))
+                other = lax.rem(mine + o, n)
+                slot = other if arriving else mine
+                action(pltpu.make_async_remote_copy(
+                    src_ref=buf.at[slot], dst_ref=buf.at[slot],
+                    send_sem=send.at[other], recv_sem=recv.at[slot],
+                    device_id={axis: other}, device_id_type=MESH,
+                ))
                 return 0
             lax.fori_loop(1, n, one, 0)
 
-    loads[0].wait()
-    gb.own(start)
-    loads[1].wait()
-    ga.own(start)
-    masks(mask_copy, start)
-    loads[2].wait()
-
-    def lane_row(v, j):
-        return jnp.broadcast_to(v[:, j : j + 1], (1, tile))
-
-    def prepare():
-        masks(mask_arrival, lambda c: c.wait_recv())
-        links = [jnp.zeros((1, tc * tile), jnp.int32) for _ in range(tr)]
-        for k in range(ka * n_col):
-            bv = bmask[k // br]
-            brow = jnp.concatenate([lane_row(bv, (k % br) * tc + j) for j in range(tc)], axis=1)
-            av = amask[k // ka]
-            for i in range(tr):
-                at = i * ka + k % ka
-                g = av[:, at : at + 1] * brow
-                gate[k * tr + i] = g.astype(jnp.float32)
-                links[i] = links[i] + g
-        for i in range(tr):
-            wrow = jnp.concatenate(
-                [jnp.broadcast_to(wp_ref[i : i + 1, j : j + 1], (1, tile)) for j in range(tc)], axis=1
-            )
-            gate[ka * n_col * tr + i] = wrow.astype(jnp.float32)
-            gate[ka * n_col * tr + tr + i] = jnp.where(links[i] > 0, wrow, 0).astype(jnp.float32)
+    masks(False, start)
+    loads[4].wait()
+    loads[5].wait()
+    for i in range(tr):
+        for j in range(tc):
+            at = (slice(i * tile, (i + 1) * tile), slice(j * tile, (j + 1) * tile))
+            m = wp_ref[i : i + 1, j : j + 1].astype(jnp.float32).astype(jnp.bfloat16)
+            wbuf[at] = wbuf[at] * m
+
+    def gather_a():
         def a_step(d, _):
             ga.line(d, True, start)
             return 0
-        lax.fori_loop(1, n_col // 2, a_step, 0)
+
         def a_across(d, _):
             ga.across(d)
             return 0
-        lax.fori_loop(0, n_col // 2, a_across, 0)
+
+        lax.fori_loop(1, ga.length, a_step, 0)
+        lax.fori_loop(0, ga.length, a_across, 0)
 
     def compute(slot):
         for bi in range(br):
@@ -226,9 +246,8 @@
             block = bbuf[slot, bi * tile : (bi + 1) * tile, :]
             for i in range(tr):
                 rows = slice(i * tile, (i + 1) * tile)
-                g = gate[k * tr + i].astype(jnp.bfloat16)
                 acc[rows, :] += jnp.dot(
-                    abuf[dev, rows, lanes], block * g, preferred_element_type=jnp.float32
+                    abuf[dev, rows, lanes], block, preferred_element_type=jnp.float32
                 )
 
     half = gb.length
@@ -239,7 +258,7 @@
         @pl.when(d == 1)
         def _():
             gb.divert(0, True, start)
-            prepare()
+            gather_a()
 
         gb.divert(d, True, start)
 
@@ -255,6 +274,11 @@
             return 0
 
         lax.fori_loop(0, 3, near, 0)
+
+        @pl.when(d == half)
+        def _():
+            masks(True, lambda c: c.wait_recv())
+
         gb.across(d - 1)
 
         def far(j, _):
@@ -272,18 +296,22 @@
 
     lax.fori_loop(1, half + 1, step, 0)
 
-    base = ka * n_col * tr
-    part = jnp.zeros((1, tc * tile), jnp.float32)
-    for i in range(tr):
-        rows = slice(i * tile, (i + 1) * tile)
-        weighted = acc[rows, :] * (wbuf[rows, :].astype(jnp.float32) * gate[base + i])
-        obuf[rows, :] = weighted.astype(jnp.bfloat16)
-        part = part + jnp.sum(weighted, axis=0, keepdims=True)
-    local_sum = jnp.sum(part, axis=1, keepdims=True)
-    count = jnp.zeros((1, 1), jnp.float32)
+    there = {}
+    links = [[jnp.zeros((1, 128), jnp.int32) for _ in range(br)] for _ in range(tr)]
+    for k in range(ka * n_col):
+        for i in range(tr):
+            at = i * ka + k % ka
+            links[i][k % br] += amask[k // ka][:, at : at + 1] * bmask[k // br]
     for i in range(tr):
         for j in range(tc):
-            count = count + gate[base + tr + i][:, j * tile : j * tile + 1]
+            link = sum(links[i][bi][:, bi * tc + j : bi * tc + j + 1] for bi in range(br))
+            there[i, j] = jnp.where(link > 0, wp_ref[i : i + 1, j : j + 1], 0).astype(jnp.float32)
+    count = sum(there.values())
+
+    weighted = acc[...] * wbuf[...].astype(jnp.float32)
+    obuf[...] = weighted.astype(jnp.bfloat16)
+    part = jnp.sum(weighted, axis=0, keepdims=True)
+    local_sum = jnp.sum(part, axis=1, keepdims=True)
     ex[me] = jnp.where(lane == 0, local_sum, jnp.where(lane == 1, count, 0.0))
 
     def ex_copy(o, mine):
@@ -308,29 +336,25 @@
         return 0
 
     lax.fori_loop(1, everyone, ex_start, 0)
-    store = pltpu.make_async_copy(obuf, masked_hbm, local_sem.at[3])
-    store.start()
 
     gb.own(wait_send)
     ga.own(wait_send)
-    masks(mask_copy, wait_send)
+    masks(False, wait_send)
+    gb.divert(0, False, wait_send)
 
     def drain_b(d, _):
         gb.line(d, False, wait_send)
         gb.divert(d, False, wait_send)
         return 0
 
-    gb.divert(0, False, wait_send)
-    lax.fori_loop(1, half + 1, drain_b, 0)
-
     def drain_a(d, _):
         ga.line(d, False, wait_send)
         return 0
 
-    lax.fori_loop(1, n_col // 2, drain_a, 0)
+    lax.fori_loop(1, half + 1, drain_b, 0)
+    lax.fori_loop(1, ga.length, drain_a, 0)
 
     lax.fori_loop(1, everyone, ex_wait, 0)
-    sums, first = jnp.zeros((1, 128), jnp.float32), jnp.zeros((1, 128), jnp.float32)
     everything = ex[...]
     order = lax.broadcasted_iota(jnp.int32, (everyone, 1, 128), 0)
     sums = jnp.sum(everything, axis=0)
@@ -339,11 +363,9 @@
     before = first[:, 1:2]
     for i in range(tr):
         for j in range(tc):
-            there = gate[base + tr + i][:, j * tile : j * tile + 1]
-            slot_ref[i : i + 1, j : j + 1] = jnp.where(there > 0, before, -1.0)
-            before = before + there
+            slot_ref[i : i + 1, j : j + 1] = jnp.where(there[i, j] > 0, before, -1.0)
+            before = before + there[i, j]
     lax.fori_loop(1, everyone, ex_done, 0)
-    store.wait()
 
 
 def on_device(a_values, a_present, b_values, b_present, w_values, w_present):
@@ -351,7 +373,6 @@
     tr, ka = a_present.shape
     br, tc = b_present.shape
     tile = a_values.shape[0] // tr
-    kt = ka * n_col
     scale = tile * math.sqrt(tr * n_row * tc * n_col)
     everyone = n_row * n_col
     dma = pltpu.SemaphoreType.DMA
@@ -364,21 +385,22 @@
             jax.ShapeDtypeStruct((tr, tc), jnp.float32),
             jax.ShapeDtypeStruct((1, 1), jnp.float32),
         ),
-        in_specs=[hbm, hbm, hbm, vmem, vmem, vmem],
-        out_specs=(hbm, vmem, vmem),
+        in_specs=[hbm] * 6,
+        out_specs=(vmem, vmem, vmem),
         scratch_shapes=[
             pltpu.VMEM((n_col, *a_values.shape), jnp.bfloat16),
             pltpu.VMEM((n_row, *b_values.shape), jnp.bfloat16),
             pltpu.VMEM(w_values.shape, jnp.bfloat16),
             pltpu.VMEM(w_values.shape, jnp.float32),
-            pltpu.VMEM(w_values.shape, jnp.bfloat16),
+            pltpu.VMEM(a_present.shape, jnp.int32),
+            pltpu.VMEM(b_present.shape, jnp.int32),
+            pltpu.VMEM(w_present.shape, jnp.int32),
             pltpu.VMEM((n_col, 1, 128), jnp.int32),
             pltpu.VMEM((n_row, 1, 128), jnp.int32),
-            pltpu.VMEM((kt * tr + 2 * tr, 1, tc * tile), jnp.float32),
             pltpu.VMEM((everyone, 1, 128), jnp.float32),
-            dma((4,)),
-            dma((3, n_col, PIECES)),
-            dma((n_col, PIECES)),
+            dma((6,)),
+            dma((3, n_col, A_PIECES)),
+            dma((n_col, A_PIECES)),
             dma((3, n_row, PIECES)),
             dma((n_row, PIECES)),
             dma((n_col,)),
@@ -387,6 +409,7 @@
             dma((n_row,)),
             dma((everyone,)),
             dma((everyone,)),
+            pltpu.SemaphoreType.REGULAR((6,)),
         ],
         compiler_params=pltpu.CompilerParams(
             collective_id=0, has_side_effects=True, vmem_limit_bytes=56 * 1024 * 1024

time: 43 us -> 40.4 us (0.940)
  Pallas kernels: 38.2 us -> 35.6 us
    pallas_call x1, Pallas kernels: 38.2 us -> 35.6 us  [on_device(): pl.pallas_call(functools.partial(kernel, n_row, n_col, tr, ka, br, tc, ti...]
where the time goes in v2:
time: 40.4 us; the launch traced here: 40.2 us
  Pallas kernels  35.6 us (88%)
  between operations  2.47 us (6%)
  local copies, waits for them, and re-layouts  2.18 us (5%)
    pallas_call x1, Pallas kernels, on_device(): pl.pallas_call(functools.partial(kernel, n_row, n_col, tr, ka, br, tc, ti...  35.6 us
    unnamed x4, local copies, waits for them, and re-layouts  2.18 us

profile of v2, /device:TPU:0, one launch (start us, length us, event | category | flops | bytes accessed | tf_op | source)
XLA Modules:
  0.0 40.2 jit_solution(16892364554095572005)
XLA Ops:
  0.6 35.6 %shard_map.85 = (bf16[256,512]{1,0:T(8,128)(2,1)}, f32[1,2]{1,0:T(1,128)}, f32[1,1]{1,0:T(1,128)}) custom-call(bf16[256,512]{1,0:T(8,128)(2,1)} %a_hbm.1, bf16[256,512]{1,0:T(8,128)(2,1)} %b_hbm.1, bf16[256,512]{1,0:T(8,128)(2,1)} %w_hbm.1, s32[1,2]{1,0:T(1,128)} %ap_hbm.1, s32[1,2]{1,0:T(1,128)} %bp_hbm.1, s32[1,2]{1,0:T(1,128)} %wp_hbm.1), custom_call_target="tpu_custom_call" | custom-call | tf_op jit(solution)/shard_map/pallas_call | solution.py:381
  36.2 0.0 copy-start
  36.2 1.7 %copy.12 = bf16[256,512]{1,0:T(8,128)(2,1)} copy(bf16[256,512]{1,0:T(8,128)(2,1)} %get-tuple-element.12) | data formatting | bytes 524288
  37.9 0.0 copy-done
  37.9 0.5 %copy.13 = f32[1,2]{1,0:T(1,128)} copy(f32[1,2]{1,0:T(1,128)S(1)} %copy-done) | data formatting | bytes 16
Async XLA Ops:
  36.2 1.7 %copy-start = (f32[1,2]{1,0:T(1,128)S(1)}, f32[1,2]{1,0:T(1,128)}, u32[]{:S(2)}) copy-start(f32[1,2]{1,0:T(1,128)} %get-tuple-element.13) | copy-start | bytes 28

commit v3 on v2

--- a/solution.py
+++ b/solution.py
@@ -109,7 +109,7 @@
 
 
 def kernel(
-    n_row, n_col, tr, ka, br, tc, tile, scale,
+    n_row, n_col, tr, ka, br, tc, tile,
     a_hbm, b_hbm, w_hbm, ap_hbm, bp_hbm, wp_hbm,
     obuf, slot_ref, total_ref,
     abuf, bbuf, wbuf, acc, ap_ref, bp_ref, wp_ref, amask, bmask, ex,
@@ -121,6 +121,17 @@
     ga = Gather("col", n_col, abuf, a_send, a_recv, A_PIECES, False)
     gb = Gather("row", n_row, bbuf, b_send, b_recv, PIECES, True)
 
+    def signal(sem, g, shift):
+        pl.semaphore_signal(sem, inc=1, device_id={g.axis: g.me + shift}, device_id_type=MESH)
+
+    barrier = pltpu.get_barrier_semaphore()
+    greeted = 0
+    for g in (gb, ga):
+        signal(barrier, g, 1 - 2 * g.side)
+        pl.when(g.can_up())(functools.partial(signal, barrier, g, 2))
+        pl.when(g.can_down())(functools.partial(signal, barrier, g, -2))
+        greeted += 1 + g.can_up().astype(jnp.int32) + g.can_down().astype(jnp.int32)
+
     pairs = (
         (bp_hbm, bp_ref), (b_hbm, bbuf.at[row]), (ap_hbm, ap_ref),
         (a_hbm, abuf.at[col]), (wp_hbm, wp_ref), (w_hbm, wbuf),
@@ -128,17 +139,6 @@
     loads = [pltpu.make_async_copy(x, y, local_sem.at[i]) for i, (x, y) in enumerate(pairs)]
     for load in loads:
         load.start()
-
-    def signal(sem, g, shift):
-        pl.semaphore_signal(sem, inc=1, device_id={g.axis: g.me + shift}, device_id_type=MESH)
-
-    barrier = pltpu.get_barrier_semaphore()
-    greeted = 0
-    for g in (gb, ga):
-        signal(barrier, g, 1 - 2 * g.side)
-        pl.when(g.can_up())(functools.partial(signal, barrier, g, 2))
-        pl.when(g.can_down())(functools.partial(signal, barrier, g, -2))
-        greeted += 1 + g.can_up().astype(jnp.int32) + g.can_down().astype(jnp.int32)
 
     def gated(get, put, present, rows, cols):
         for i in range(rows):
@@ -314,28 +314,25 @@
     local_sum = jnp.sum(part, axis=1, keepdims=True)
     ex[me] = jnp.where(lane == 0, local_sum, jnp.where(lane == 1, count, 0.0))
 
-    def ex_copy(o, mine):
-        other = lax.rem(me + o, everyone)
-        slot = me if mine else other
-        return pltpu.make_async_remote_copy(
-            src_ref=ex.at[slot], dst_ref=ex.at[slot],
-            send_sem=ex_send.at[other], recv_sem=ex_recv.at[slot],
-            device_id=(other // n_col, lax.rem(other, n_col)), device_id_type=MESH,
-        )
-
     def ex_start(o, _):
-        ex_copy(o, True).start()
+        other = jnp.where(me < everyone // 2, everyone - 1 - o, o)
+
+        @pl.when(other != me)
+        def _():
+            pltpu.make_async_remote_copy(
+                src_ref=ex.at[me], dst_ref=ex.at[me],
+                send_sem=ex_send.at[0], recv_sem=ex_recv.at[0],
+                device_id=(other // n_col, lax.rem(other, n_col)), device_id_type=MESH,
+            ).start()
         return 0
 
-    def ex_wait(o, _):
-        ex_copy(o, False).wait_recv()
-        return 0
-
-    def ex_done(o, _):
-        ex_copy(o, True).wait_send()
-        return 0
-
-    lax.fori_loop(1, everyone, ex_start, 0)
+    rest = ex.at[pl.ds(0, everyone - 1)]
+    ex_all = pltpu.make_async_remote_copy(
+        src_ref=rest, dst_ref=rest, send_sem=ex_send.at[0], recv_sem=ex_recv.at[0],
+        device_id={"col": col + 1 - 2 * ga.side}, device_id_type=MESH,
+    )
+
+    lax.fori_loop(0, everyone, ex_start, 0)
 
     gb.own(wait_send)
     ga.own(wait_send)
@@ -354,18 +351,24 @@
     lax.fori_loop(1, half + 1, drain_b, 0)
     lax.fori_loop(1, ga.length, drain_a, 0)
 
-    lax.fori_loop(1, everyone, ex_wait, 0)
+    ex_all.wait_recv()
     everything = ex[...]
     order = lax.broadcasted_iota(jnp.int32, (everyone, 1, 128), 0)
     sums = jnp.sum(everything, axis=0)
     first = jnp.sum(jnp.where(order < me, everything, 0.0), axis=0)
-    total_ref[...] = sums[:, 0:1] / scale
+    total_ref[...] = jnp.where(lane == 0, sums, 0.0)
     before = first[:, 1:2]
     for i in range(tr):
         for j in range(tc):
-            slot_ref[i : i + 1, j : j + 1] = jnp.where(there[i, j] > 0, before, -1.0)
+            slot_ref[i : i + 1, j : j + 1] = jnp.where(there[i, j] > 0, before + 1.0, 0.0)
             before = before + there[i, j]
-    lax.fori_loop(1, everyone, ex_done, 0)
+    ex_all.wait_send()
+
+
+def finish(scale, masked_in, slot_in, total_in, masked_ref, slot_ref, total_ref):
+    masked_ref[...] = masked_in[...]
+    slot_ref[...] = slot_in[...] - 1.0
+    total_ref[...] = total_in[:, 0:1] / scale
 
 
 def on_device(a_values, a_present, b_values, b_present, w_values, w_present):
@@ -379,11 +382,11 @@
     hbm = pl.BlockSpec(memory_space=pl.ANY)
     vmem = pl.BlockSpec(memory_space=pltpu.VMEM)
     masked, slot, total = pl.pallas_call(
-        functools.partial(kernel, n_row, n_col, tr, ka, br, tc, tile, scale),
+        functools.partial(kernel, n_row, n_col, tr, ka, br, tc, tile),
         out_shape=(
             jax.ShapeDtypeStruct(w_values.shape, jnp.bfloat16),
             jax.ShapeDtypeStruct((tr, tc), jnp.float32),
-            jax.ShapeDtypeStruct((1, 1), jnp.float32),
+            jax.ShapeDtypeStruct((1, 128), jnp.float32),
         ),
         in_specs=[hbm] * 6,
         out_specs=(vmem, vmem, vmem),
@@ -407,14 +410,25 @@
             dma((n_col,)),
             dma((n_row,)),
             dma((n_row,)),
-            dma((everyone,)),
-            dma((everyone,)),
+            dma((1,)),
+            dma((1,)),
             pltpu.SemaphoreType.REGULAR((6,)),
         ],
         compiler_params=pltpu.CompilerParams(
             collective_id=0, has_side_effects=True, vmem_limit_bytes=56 * 1024 * 1024
         ),
     )(a_values, b_values, w_values, a_present, b_present, w_present)
+    masked, slot, total = pl.pallas_call(
+        functools.partial(finish, scale),
+        out_shape=(
+            jax.ShapeDtypeStruct(masked.shape, masked.dtype),
+            jax.ShapeDtypeStruct(slot.shape, slot.dtype),
+            jax.ShapeDtypeStruct((1, 1), jnp.float32),
+        ),
+        in_specs=[vmem] * 3,
+        out_specs=(vmem, vmem, vmem),
+        compiler_params=pltpu.CompilerParams(vmem_limit_bytes=16 * 1024 * 1024),
+    )(masked, slot, total)
     return masked, slot, total.reshape(())
 
 

time: 40.4 us -> 37.9 us (0.938)
  between operations: 2.47 us -> 0.66 us
  local copies, waits for them, and re-layouts: 2.18 us -> 1.55 us
    pallas_call x1, Pallas kernels: 35.6 us -> 34.8 us  [on_device(): pl.pallas_call(functools.partial(kernel, n_row, n_col, tr, ka, br, tc, ti...]
    pallas_call x0 -> x1, Pallas kernels: none -> 0.73 us  [on_device(): pl.pallas_call(functools.partial(finish, scale), out_shape=(jax.ShapeDtyp...]
    unnamed x4 -> x6, local copies, waits for them, and re-layouts: 2.18 us -> 1.55 us
where the time goes in v3:
time: 37.9 us; the launch traced here: 37.7 us
  Pallas kernels  35.5 us (94%)
  local copies, waits for them, and re-layouts  1.55 us (4%)
  between operations  0.66 us (2%)
    pallas_call x1, Pallas kernels, on_device(): pl.pallas_call(functools.partial(kernel, n_row, n_col, tr, ka, br, tc, ti...  34.8 us
    unnamed x6, local copies, waits for them, and re-layouts  1.55 us

profile of v3, /device:TPU:0, one launch (start us, length us, event | category | flops | bytes accessed | tf_op | source)
XLA Modules:
  0.0 37.7 jit_solution(17896484126654220306)
XLA Ops:
  0.6 34.8 %shard_map.85 = (bf16[256,512]{1,0:T(8,128)(2,1)}, f32[1,2]{1,0:T(1,128)}, f32[1,128]{1,0:T(1,128)}) custom-call(bf16[256,512]{1,0:T(8,128)(2,1)} %a_hbm.1, bf16[256,512]{1,0:T(8,128)(2,1)} %b_hbm.1, bf16[256,512]{1,0:T(8,128)(2,1)} %w_hbm.1, s32[1,2]{1,0:T(1,128)} %ap_hbm.1, s32[1,2]{1,0:T(1,128)} %bp_hbm.1, s32[1,2]{1,0:T(1,128)} %wp_hbm.1), custom_call_target="tpu_custom_call" | custom-call | tf_op jit(solution)/shard_map/pallas_call | solution.py:384
  35.4 0.0 copy-start.1
  35.4 0.0 copy-start.2
  35.4 0.6 %copy-done.1 = f32[1,2]{1,0:T(1,128)S(1)} copy-done((f32[1,2]{1,0:T(1,128)S(1)}, f32[1,2]{1,0:T(1,128)}, u32[]{:S(2)}) %copy-start.1) | copy-done | bytes 32
  36.0 0.0 copy-done.2
  36.0 0.0 copy-start
  36.0 0.9 %copy-done = bf16[256,512]{1,0:T(8,128)(2,1)S(1)} copy-done((bf16[256,512]{1,0:T(8,128)(2,1)S(1)}, bf16[256,512]{1,0:T(8,128)(2,1)}, u32[]{:S(2)}) %copy-start) | copy-done | bytes 262168
  37.0 0.7 %shard_map.86 = (bf16[256,512]{1,0:T(8,128)(2,1)}, f32[1,2]{1,0:T(1,128)}, f32[1,1]{1,0:T(1,128)}) custom-call(bf16[256,512]{1,0:T(8,128)(2,1)S(1)} %copy-done, f32[1,2]{1,0:T(1,128)S(1)} %copy-done.1, f32[1,128]{1,0:T(1,128)S(1)} %copy-done.2), custom_call_target="tpu_custom_call" | custom-call | tf_op jit(solution)/shard_map/pallas_call | solution.py:421
Async XLA Ops:
  35.4 0.6 %copy-start.1 = (f32[1,2]{1,0:T(1,128)S(1)}, f32[1,2]{1,0:T(1,128)}, u32[]{:S(2)}) copy-start(f32[1,2]{1,0:T(1,128)} %get-tuple-element.10.slot_in) | copy-start | bytes 28
  35.4 0.6 %copy-start.2 = (f32[1,128]{1,0:T(1,128)S(1)}, f32[1,128]{1,0:T(1,128)}, u32[]{:S(2)}) copy-start(f32[1,128]{1,0:T(1,128)} %get-tuple-element.11.total_in) | copy-start | bytes 1540
  36.0 0.9 %copy-start = (bf16[256,512]{1,0:T(8,128)(2,1)S(1)}, bf16[256,512]{1,0:T(8,128)(2,1)}, u32[]{:S(2)}) copy-start(bf16[256,512]{1,0:T(8,128)(2,1)} %get-tuple-element.9.masked_in) | copy-start | bytes 786436

commit v4 on v3

--- a/solution.py
+++ b/solution.py
@@ -384,9 +384,9 @@
     masked, slot, total = pl.pallas_call(
         functools.partial(kernel, n_row, n_col, tr, ka, br, tc, tile),
         out_shape=(
-            jax.ShapeDtypeStruct(w_values.shape, jnp.bfloat16),
-            jax.ShapeDtypeStruct((tr, tc), jnp.float32),
-            jax.ShapeDtypeStruct((1, 128), jnp.float32),
+            pltpu.VMEM(w_values.shape, jnp.bfloat16),
+            pltpu.VMEM((tr, tc), jnp.float32),
+            pltpu.VMEM((1, 128), jnp.float32),
         ),
         in_specs=[hbm] * 6,
         out_specs=(vmem, vmem, vmem),

time: 37.9 us -> 35.6 us (0.939)
  local copies, waits for them, and re-layouts: 1.55 us -> 0 us
  Pallas kernels: 35.5 us -> 34.8 us
    unnamed x6 -> x0, local copies, waits for them, and re-layouts: 1.55 us -> none
    pallas_call x1, Pallas kernels: 34.8 us -> 34 us  [on_device(): pl.pallas_call(functools.partial(kernel, n_row, n_col, tr, ka, br, tc, ti...]
where the time goes in v4:
time: 35.6 us; the launch traced here: 35.4 us
  Pallas kernels  34.8 us (98%)
  between operations  0.64 us (2%)
    pallas_call x1, Pallas kernels, on_device(): pl.pallas_call(functools.partial(kernel, n_row, n_col, tr, ka, br, tc, ti...  34 us
    pallas_call x1, Pallas kernels, on_device(): pl.pallas_call(functools.partial(finish, scale), out_shape=(jax.ShapeDtyp...  0.73 us

profile of v4, /device:TPU:0, one launch (start us, length us, event | category | flops | bytes accessed | tf_op | source)
XLA Modules:
  0.0 35.4 jit_solution(15883577748878067955)
XLA Ops:
  0.6 34.0 %shard_map.85 = (bf16[256,512]{1,0:T(8,128)(2,1)S(1)}, f32[1,2]{1,0:T(1,128)S(1)}, f32[1,128]{1,0:T(1,128)S(1)}) custom-call(bf16[256,512]{1,0:T(8,128)(2,1)} %a_hbm.1, bf16[256,512]{1,0:T(8,128)(2,1)} %b_hbm.1, bf16[256,512]{1,0:T(8,128)(2,1)} %w_hbm.1, s32[1,2]{1,0:T(1,128)} %ap_hbm.1, s32[1,2]{1,0:T(1,128)} %bp_hbm.1, s32[1,2]{1,0:T(1,128)} %wp_hbm.1), custom_call_target="tpu_custom_call" | custom-call | tf_op jit(solution)/shard_map/pallas_call | solution.py:384
  34.7 0.7 %shard_map.86 = (bf16[256,512]{1,0:T(8,128)(2,1)}, f32[1,2]{1,0:T(1,128)}, f32[1,1]{1,0:T(1,128)}) custom-call(bf16[256,512]{1,0:T(8,128)(2,1)S(1)} %get-tuple-element.9.masked_in, f32[1,2]{1,0:T(1,128)S(1)} %get-tuple-element.10.slot_in, f32[1,128]{1,0:T(1,128)S(1)} %get-tuple-element.11.total_in), custom_call_target="tpu_custom_call" | custom-call | tf_op jit(solution)/shard_map/pallas_call | solution.py:421
